TPU v7x, 32 devices: a whole 2x2x4 slice. The times are simulated.
32 devices in a mesh: dp: 8 (over z, y), expert: 4 (over x, core).
Axes of the slice: x: 2, y: 2, z: 4, core: 2. Of those that a mesh axis runs over, the one named last changes fastest.
Arguments:
- expert_grads: bfloat16 [8, 4, 1024, 896], P('dp', 'expert'), may hold values from -768 to 768
- round_offsets: int32 [8, 4, 1024], P('dp', 'expert'), may hold values from 0 to 1073741823
- slot_expert: int32 [4], replicated, may hold values from 0 to 3, each once
- master_weight: float32 [4, 1024, 896], P('expert', 'dp'), may hold values from -0.1875 to 0.1875
Outputs:
- mean_grad: float32 [4, 1024, 896], P('expert', 'dp')
- new_weight: float32 [4, 1024, 896], P('expert', 'dp')
- block_step: float32 [4, 8], P('expert', 'dp')
Inputs may be any that keep to these rules, and one draw needn't show every extreme that they name: `slot_expert`: each of 0 to 3 appears once.
All inputs are finite; a program needn't handle non-finite values.
Results may differ from a plain program's by a relative error of at most 0.0003.
Values may be sent and summed in bfloat16 or wider, within the bound.
A program may use at most 64 MiB of HBM per device.

v0:
```python
import jax
import jax.numpy as jnp
from jax import lax
from jax.sharding import PartitionSpec as P

level_bits = 6
low_power = -30
high_power = 30
learn_rate = 0.05
field_base = 32768
count_shift = 64


def power_steps(maxima):
    powers = jnp.array([2.0**exponent for exponent in range(low_power, high_power)], jnp.float32)
    reached = maxima[..., None] >= powers
    doubled = jnp.prod(jnp.where(reached, jnp.float32(2.0), jnp.float32(1.0)), axis=-1)
    return 2.0 ** (low_power - level_bits) * doubled


def dither(element_code):
    mixed = element_code * 747796405 + 1013904223
    mixed = jnp.bitwise_xor(mixed, jnp.right_shift(mixed, 13))
    mixed = mixed * 1103515245
    mixed = jnp.bitwise_xor(mixed, jnp.right_shift(mixed, 16))
    return jnp.bitwise_and(jnp.right_shift(mixed, 12), 255).astype(jnp.float32) / 256.0


def quantize(values, inverse_step, offsets):
    columns = lax.broadcasted_iota(jnp.int32, (1, values.shape[-1]), 1)
    element_code = offsets[..., None] + columns
    scaled = values * inverse_step
    floor_part = jnp.floor(scaled)
    return (floor_part + jnp.floor(scaled - floor_part + dither(element_code))).astype(jnp.int32)


def local_counts(local_grads, round_offsets, all_steps, dp_count):
    slot_count = local_grads.shape[0]
    row_count = local_grads.shape[1]
    hidden = local_grads.shape[2]
    block_rows = row_count // dp_count
    shaped = local_grads.reshape(slot_count, dp_count, block_rows, hidden)
    offsets_shaped = round_offsets[0].reshape(slot_count, dp_count, block_rows)
    counts = quantize(
        shaped.astype(jnp.float32), (1.0 / all_steps)[:, :, None, None], offsets_shaped
    )
    return counts.reshape(slot_count, row_count, hidden)


def block_peaks(local_grads, dp_count):
    slot_count = local_grads.shape[0]
    row_count = local_grads.shape[1]
    hidden = local_grads.shape[2]
    shaped = local_grads.reshape(slot_count, dp_count, row_count // dp_count, hidden)
    return jnp.max(jnp.abs(shaped), axis=(2, 3)).astype(jnp.float32)


def body(expert_grads, round_offsets, slot_expert, master_weight):
    dp_count = lax.axis_size("dp")
    local_grads = expert_grads[0]
    slot_count = local_grads.shape[0]
    hidden = local_grads.shape[2]
    maxima = lax.pmax(block_peaks(local_grads, dp_count), "dp")
    all_steps = power_steps(maxima)
    counts = local_counts(local_grads, round_offsets, all_steps, dp_count)
    half = hidden // 2
    words = (counts[:, :, :half] + count_shift) * field_base + (counts[:, :, half:] + count_shift)
    summed = lax.psum_scatter(words, "dp", scatter_dimension=1, tiled=True)
    upper = jnp.right_shift(summed, 15) - count_shift * dp_count
    lower = jnp.bitwise_and(summed, field_base - 1) - count_shift * dp_count
    totals = jnp.concatenate([upper, lower], axis=2)
    step_sizes = lax.dynamic_slice_in_dim(all_steps, lax.axis_index("dp"), 1, 1)
    mean_slot = totals.astype(jnp.float32) * (step_sizes / dp_count)[..., None]
    gathered, gathered_steps = (
        lax.all_gather(mean_slot, "expert", axis=0, tiled=True),
        lax.all_gather(step_sizes, "expert", axis=0, tiled=True),
    )
    wanted = lax.axis_index("expert") * slot_count + lax.broadcasted_iota(
        jnp.int32, (slot_count, 1), 0
    )
    positions = lax.broadcasted_iota(jnp.int32, (1, slot_expert.shape[0]), 1)
    holder = jnp.sum(jnp.where(slot_expert[None, :] == wanted, positions, 0), axis=1)
    mean_grad = gathered[holder]
    block_step = gathered_steps[holder]
    new_weight = master_weight - learn_rate * mean_grad
    return (mean_grad, new_weight, block_step)


def solution(mesh):
    return jax.shard_map(
        body,
        mesh=mesh,
        in_specs=(
            P("dp", "expert", None, None),
            P("dp", "expert", None),
            P(),
            P("expert", "dp", None),
        ),
        out_specs=(P("expert", "dp", None), P("expert", "dp", None), P("expert", "dp")),
        check_vma=False,
    )
```

profile of v0, /device:TPU:0, one launch (start us, length us, event | category | flops | bytes accessed | tf_op | source)
XLA Modules:
  0.0 170.6 jit_solution(9877344274408104898)
XLA Ops:
  7.2 0.0 all-reduce.4.cloned.1.call-start
  7.2 1.9 %abs_reduce_fusion = bf16[1024]{0:T(1024)(128)(2,1)S(1)} fusion(bf16[1,1,1024,896]{3,2,1,0:T(8,128)(2,1)} %param.5), kind=kLoop, calls=%fused_computation.17 | loop fusion | flops 1833984 | bytes 1837056 | tf_op jit(solution)/shard_map/reduce_max | solution.py:55
  9.2 0.1 bitcast_reduce_fusion
  9.3 23.2 %pmax.10 = f32[8]{0:T(128)S(1)} all-reduce(bf16[8]{0:T(256)(128)(2,1)S(1)} %bitcast_reduce_fusion), channel_id=1, replica_groups=mesh['dp'=8,'expert'=4] {'dp'}, use_global_device_ids=true, to_apply=%region_2.3 | all-reduce | flops 8 | bytes 48 | tf_op jit(solution)/shard_map/pmax | solution.py:63
  32.4 0.8 select_reduce_fusion
  33.3 0.1 broadcast_bitcast_fusion
  33.3 4.2 %fusion.2 = s32[1,1024,896]{2,1,0:T(8,128)S(1)} fusion(bf16[1,1,1024,896]{3,2,1,0:T(8,128)(2,1)} %param.5, s32[1024]{0:T(1024)} %bitcast.18, f32[1024]{0:T(1024)S(1)} %broadcast_bitcast_fusion), kind=kLoop, calls=%fused_computation.6 | loop fusion | flops 18350080 | bytes 5513216 | tf_op jit(solution)/shard_map/convert_element_type | solution.py:34
  37.5 0.0 copy-start.3
  37.5 1.9 %fusion.8 = s32[1,1024,448]{2,1,0:T(8,128)} fusion(s32[1,1024,896]{2,1,0:T(8,128)S(1)} %fusion.2), kind=kLoop, calls=%fused_computation.14 | loop fusion | flops 1835008 | bytes 5505024 | tf_op jit(solution)/shard_map/add | solution.py:67
  39.5 0.0 all-reduce.4.cloned.1.call-update
  39.5 0.0 all-gather.3.cloned.1.call-start
  39.6 0.6 dynamic-slice.14
  40.8 0.6 dynamic-slice.3
  42.0 97.2 %all-reduce.4.cloned.1.call-done = s32[1,1024,448]{2,1,0:T(8,128)} async-done(((s32[1,1024,448]{2,1,0:T(8,128)}), s32[1,1024,448]{2,1,0:T(8,128)}) %all-reduce.4.cloned.1.call-update) | async-done | bytes 1835024
  139.2 1.0 shift-right-arithmetic_add_fusion
  140.2 0.9 fusion.10
  141.1 0.0 all-gather.3.cloned.1.call-update
  141.2 0.6 dynamic-slice.13
  141.8 1.4 dynamic-update-slice.2
  143.2 6.1 %all-reduce = f32[4]{0:T(128)S(1)} all-reduce(f32[4]{0:T(128)S(1)} %dynamic-update-slice.2), channel_id=2, replica_groups=mesh['dp'=8,'expert'=4] {'expert'}, use_global_device_ids=true, to_apply=%add | all-reduce | flops 4 | bytes 32
  149.3 0.6 fusion.11
  151.9 0.6 dynamic-slice.12
  152.4 9.3 %all-gather.3.cloned.1.call-done = f32[4,128,896]{2,1,0:T(8,128)} async-done(((f32[1,128,896]{2,1,0:T(8,128)}), f32[4,128,896]{2,1,0:T(8,128)}) %all-gather.3.cloned.1.call-update) | async-done | bytes 1835024 | tf_op jit(solution)/shard_map/all_gather | solution.py:75
  161.8 2.0 %multiply_subtract_fusion = (f32[1,128,896]{2,1,0:T(8,128)}, f32[1,128,896]{2,1,0:T(8,128)}) fusion(f32[1,128,896]{2,1,0:T(8,128)S(1)} %copy-done, f32[4,128,896]{2,1,0:T(8,128)} %all-gather.3.cloned.1.call-done, s32[]{:T(128)} %bitcast.11), kind=kLoop, calls=%fused_computation.20 | loop fusion | flops 229376 | bytes 1835012 | tf_op jit(solution)/shard_map/sub | solution.py:85
  (9 shorter events, 0.0 us)
Async XLA Ops:
  7.2 132.0 %all-reduce.4.cloned.1.call-start = ((), (), s32[]{:S(2)}) async-start(), calls=%async_computation.1 | async-start | bytes 4194304
  37.5 2.0 %copy-start.3 = (u32[32]{0:T(128)S(1)}, u32[32]{0:T(128)}, u32[]{:S(2)}) copy-start(u32[32]{0:T(128)} %constant.113) | copy-start | bytes 388
  39.5 101.7 %copy-start.2 = (u32[32]{0:T(128)S(1)}, u32[32]{0:T(128)}, u32[]{:S(2)}) copy-start(u32[32]{0:T(128)} %constant.107) | copy-start | bytes 388
  39.5 109.8 %copy-start.1 = (s32[4]{0:T(128)S(1)}, s32[4]{0:T(128)}, u32[]{:S(2)}) copy-start(s32[4]{0:T(128)} %param.7) | copy-start | bytes 52
  39.5 122.3 %copy-start = (f32[1,128,896]{2,1,0:T(8,128)S(1)}, f32[1,128,896]{2,1,0:T(8,128)}, u32[]{:S(2)}) copy-start(f32[1,128,896]{2,1,0:T(8,128)} %param.8) | copy-start | bytes 1376260
  39.5 122.3 %all-gather.3.cloned.1.call-start = ((), (), s32[]{:S(2)}) async-start(), calls=%async_computation | async-start | bytes 2293760 | tf_op jit(solution)/shard_map/all_gather | solution.py:75
Sparse Core Ops, SparseCore 0:
  39.6 99.5 all-reduce.3
  141.3 20.3 all-gather.2
where the time goes:
time: 171 us
  waiting for transfers between devices  107 us (63%)
  blocking collectives  29.3 us (17%)
  between operations  17.4 us (10%)
  other arithmetic  13.5 us (8%)
  local copies, waits for them, and re-layouts  3.84 us (2%)
    unnamed x3, waiting for transfers between devices  97.2 us
    pmax x1, blocking collectives, body(): maxima = lax.pmax(block_peaks(local_grads, dp_count), 'dp')  23.2 us
    all_gather x1, waiting for transfers between devices, body(): lax.all_gather(mean_slot, 'expert', axis=0, tiled=True)  9.31 us
    unnamed x1, blocking collectives  6.11 us
    convert_element_type x1, other arithmetic, quantize(): (floor_part + jnp.floor(scaled - floor_part + dither(element_code))).asty...  4.18 us
  transfers between devices with their start and end apart: 2, of which 2 were waited for; matrix products, arithmetic and copies ran while one was open for 3% of the time, Pallas kernels for 0%

commit v1 on v0

--- a/solution.py
+++ b/solution.py
@@ -1,6 +1,10 @@
+import functools
+
 import jax
 import jax.numpy as jnp
 from jax import lax
+from jax.experimental import pallas as pl
+from jax.experimental.pallas import tpu as pltpu
 from jax.sharding import PartitionSpec as P
 
 level_bits = 6
@@ -86,9 +90,363 @@
     return (mean_grad, new_weight, block_step)
 
 
+lanes = 128
+chunk_rows = 16
+MESH = pl.DeviceIdType.MESH
+
+
+def mixed_dither(code):
+    mixed = jnp.bitwise_xor(code, jnp.right_shift(code, 13))
+    mixed = mixed * 1103515245
+    mixed = jnp.bitwise_xor(mixed, jnp.right_shift(mixed, 16))
+    return jnp.bitwise_and(jnp.right_shift(mixed, 12), 255).astype(jnp.float32) * (1.0 / 256.0)
+
+
+def exchange_kernel(
+    n_dp,
+    n_expert,
+    slots_ref,
+    grads_ref,
+    offs_ref,
+    total_ref,
+    step_ref,
+    own,
+    peer_raw,
+    peer_offs,
+    codes,
+    my_max,
+    max_in,
+    inverse,
+    my_step,
+    step_in,
+    stage,
+    z_in,
+    x_out,
+    x_in,
+    load_sem,
+    y_send,
+    y_recv,
+    z_send,
+    z_recv,
+    x_send,
+    x_recv,
+    m_send,
+    m_recv,
+    o_send,
+    o_recv,
+    s_send,
+    s_recv,
+):
+    lead = n_dp // 2
+    block_rows = own.shape[1]
+    hidden = own.shape[2]
+    tiles = hidden // lanes
+    chunks = block_rows // chunk_rows
+    me = lax.axis_index("dp")
+    mine = lax.axis_index("expert")
+    row = lax.div(me, 2)
+    side = lax.rem(me, 2)
+    partner = me + 1 - 2 * side
+
+    def rows_of(c):
+        return pl.ds(pl.multiple_of(c * chunk_rows, chunk_rows), chunk_rows)
+
+    def dp_peer(d):
+        return lax.rem(me + d, n_dp)
+
+    def row_peer(d):
+        return lax.rem(row + d, lead)
+
+    def expert_peer(d):
+        return lax.rem(mine + d, n_expert)
+
+    def load_copy(b):
+        return pltpu.make_async_copy(
+            grads_ref.at[lax.div(b, 2), lax.rem(b, 2)], own.at[b], load_sem.at[b]
+        )
+
+    def remote(src, dst, send, recv, dp, expert):
+        return pltpu.make_async_remote_copy(
+            src_ref=src,
+            dst_ref=dst,
+            send_sem=send,
+            recv_sem=recv,
+            device_id=(dp, expert),
+            device_id_type=MESH,
+        )
+
+    def y_copy(c):
+        return remote(
+            grads_ref.at[:, 1 - side, rows_of(c), :],
+            peer_raw.at[c],
+            y_send.at[c],
+            y_recv.at[c],
+            partner,
+            mine,
+        )
+
+    def z_copy(d, c):
+        return remote(
+            stage.at[d, rows_of(c), :],
+            z_in.at[d - 1, rows_of(c), :],
+            z_send.at[d - 1, c],
+            z_recv.at[d - 1, c],
+            row_peer(d) * 2 + side,
+            mine,
+        )
+
+    def x_copy(d, c):
+        return remote(
+            x_out.at[rows_of(c), :],
+            x_in.at[d - 1, rows_of(c), :],
+            x_send.at[d - 1, c],
+            x_recv.at[d - 1, c],
+            me,
+            expert_peer(d),
+        )
+
+    def m_copy(d):
+        return remote(
+            my_max, max_in.at[d - 1], m_send.at[d - 1], m_recv.at[d - 1], dp_peer(d), mine
+        )
+
+    def s_copy(d):
+        return remote(
+            my_step, step_in.at[d - 1], s_send.at[d - 1], s_recv.at[d - 1], me, expert_peer(d)
+        )
+
+    o_copy = remote(offs_ref, peer_offs, o_send, o_recv, partner, mine)
+
+    for b in range(n_dp):
+        load_copy(b).start()
+    barrier = pltpu.get_barrier_semaphore()
+    for d in range(1, n_dp):
+        pl.semaphore_signal(barrier, inc=1, device_id=(dp_peer(d), mine), device_id_type=MESH)
+    for d in range(1, n_expert):
+        pl.semaphore_signal(barrier, inc=1, device_id=(me, expert_peer(d)), device_id_type=MESH)
+
+    block_of_row = lax.broadcasted_iota(jnp.int32, (n_dp, lanes), 0)
+    peaks = jnp.zeros((n_dp, lanes), jnp.float32)
+    for b in range(n_dp):
+        load_copy(b).wait()
+
+        def peak_rows(i, peak):
+            return jnp.maximum(peak, jnp.abs(own[b, rows_of(i), :]))
+
+        peak = lax.fori_loop(
+            0, chunks, peak_rows, jnp.zeros((chunk_rows, hidden), own.dtype), unroll=True
+        ).astype(jnp.float32)
+        peak = jnp.max(jnp.max(peak, axis=0, keepdims=True), axis=1, keepdims=True)
+        peaks = jnp.where(block_of_row == b, peak, peaks)
+    my_max[...] = peaks
+
+    pl.semaphore_wait(barrier, n_dp + n_expert - 2)
+    for d in range(1, n_dp):
+        m_copy(d).start()
+    o_copy.start()
+    for c in range(chunks):
+        y_copy(c).start()
+
+    def spread(source, slot):
+        lines = source[...]
+        for k in range(lead):
+            line = jnp.where(side == 0, lines[2 * k : 2 * k + 1], lines[2 * k + 1 : 2 * k + 2])
+            column = jnp.transpose(jnp.broadcast_to(line, (lanes, block_rows)))
+            codes[slot, k] = column * 747796405 + 1013904223
+
+    spread(offs_ref, 0)
+    o_copy.wait_recv()
+    spread(peer_offs, 1)
+
+    peak = my_max[...]
+    for d in range(1, n_dp):
+        m_copy(d).wait_recv()
+        peak = jnp.maximum(peak, max_in[d - 1])
+    step = jnp.full(peak.shape, 2.0 ** (low_power - level_bits), jnp.float32)
+    inv = jnp.full(peak.shape, 2.0 ** (level_bits - low_power), jnp.float32)
+    for k in range(low_power, high_power):
+        reached = peak >= 2.0**k
+        step = jnp.where(reached, 2.0 ** (k + 1 - level_bits), step)
+        inv = jnp.where(reached, 2.0 ** (level_bits - k - 1), inv)
+    my_step[...] = step
+    for b in range(n_dp):
+        inverse[b] = jnp.broadcast_to(inv[b : b + 1], (chunk_rows, lanes))
+
+    columns = lax.broadcasted_iota(jnp.int32, (chunk_rows, hidden), 1) * 747796405
+
+    def quantized(values, inv_row, code):
+        scaled = values.astype(jnp.float32) * inv_row
+        floor_part = jnp.floor(scaled)
+        wide = jnp.concatenate([code] * tiles, axis=1)
+        return floor_part + jnp.floor((scaled - floor_part) + mixed_dither(wide + columns))
+
+    def round_and_send(c):
+        y_copy(c).wait_recv()
+
+        def one(i, carry):
+            d = lax.rem(i + 1, lead)
+            k = row_peer(d)
+            b = 2 * k + side
+            inv_row = jnp.concatenate([inverse[b]] * tiles, axis=1)
+            here = quantized(own[b, rows_of(c), :], inv_row, codes[0, k, rows_of(c), :])
+            there = quantized(peer_raw[c, k], inv_row, codes[1, k, rows_of(c), :])
+            stage[d, rows_of(c), :] = (here + there).astype(stage.dtype)
+            return carry
+
+        lax.fori_loop(0, lead, one, 0)
+        for d in range(1, lead):
+            z_copy(d, c).start()
+
+    def add_and_send(c):
+        total = stage[0, rows_of(c), :].astype(jnp.float32)
+        for d in range(1, lead):
+            z_copy(d, c).wait_recv()
+            total = total + z_in[d - 1, rows_of(c), :].astype(jnp.float32)
+        x_out[rows_of(c), :] = total.astype(jnp.int32).astype(x_out.dtype)
+        for d in range(1, n_expert):
+            x_copy(d, c).start()
+
+    def weight_of(slot):
+        return jnp.where(slots_ref[slot] == mine, jnp.float32(1.0), jnp.float32(0.0))
+
+    weights = [weight_of(lax.rem(mine + n_expert - d, n_expert)) for d in range(n_expert)]
+
+    def select(c):
+        chosen = x_out[rows_of(c), :].astype(jnp.int32).astype(jnp.float32) * weights[0]
+        for d in range(1, n_expert):
+            x_copy(d, c).wait_recv()
+            part = x_in[d - 1, rows_of(c), :].astype(jnp.int32).astype(jnp.float32)
+            chosen = chosen + part * weights[d]
+        total_ref[rows_of(c), :] = chosen
+
+    lag_add = min(2, chunks)
+    lag_select = min(3, chunks)
+    for t in range(chunks + lag_select):
+        if t < chunks:
+            round_and_send(t)
+        if t == 0:
+            for d in range(1, n_expert):
+                s_copy(d).start()
+        if 0 <= t - lag_add < chunks:
+            add_and_send(t - lag_add)
+        if 0 <= t - lag_select < chunks:
+            select(t - lag_select)
+
+    chosen_step = my_step[...] * weights[0]
+    for d in range(1, n_expert):
+        s_copy(d).wait_recv()
+        chosen_step = chosen_step + step_in[d - 1] * weights[d]
+    held = jnp.where(block_of_row == me, chosen_step, 0.0)
+    step_ref[...] = jnp.broadcast_to(jnp.max(held, axis=0, keepdims=True), held.shape)
+
+    for d in range(1, n_dp):
+        m_copy(d).wait_send()
+    o_copy.wait_send()
+    for d in range(1, n_expert):
+        s_copy(d).wait_send()
+    for c in range(chunks):
+        y_copy(c).wait_send()
+        for d in range(1, lead):
+            z_copy(d, c).wait_send()
+        for d in range(1, n_expert):
+            x_copy(d, c).wait_send()
+
+
+def apply_kernel(n_dp, total_ref, step_ref, master_ref, mean_ref, weight_ref, block_step_ref):
+    step = step_ref[0:1, 0:1]
+    mean = total_ref[...] * (step / n_dp)
+    mean_ref[0] = mean
+    weight_ref[0] = master_ref[0] - learn_rate * mean
+    block_step_ref[...] = step
+
+
+def exchange_body(n_dp, n_expert, expert_grads, round_offsets, slot_expert, master_weight):
+    row_count, hidden = expert_grads.shape[2:]
+    lead = n_dp // 2
+    block_rows = row_count // n_dp
+    chunks = block_rows // chunk_rows
+    grads = expert_grads.reshape(lead, 2, block_rows, hidden)
+    offs = round_offsets.reshape(n_dp, block_rows)
+    dma = pltpu.SemaphoreType.DMA
+    bf16 = jnp.bfloat16
+    vmem = pl.BlockSpec(memory_space=pltpu.VMEM)
+    totals, steps = pl.pallas_call(
+        functools.partial(exchange_kernel, n_dp, n_expert),
+        out_shape=(
+            jax.ShapeDtypeStruct((block_rows, hidden), jnp.float32),
+            jax.ShapeDtypeStruct((n_dp, lanes), jnp.float32),
+        ),
+        in_specs=[
+            pl.BlockSpec(memory_space=pltpu.SMEM),
+            pl.BlockSpec(memory_space=pl.ANY),
+            vmem,
+        ],
+        out_specs=(vmem, vmem),
+        scratch_shapes=[
+            pltpu.VMEM((n_dp, block_rows, hidden), bf16),
+            pltpu.VMEM((chunks, lead, chunk_rows, hidden), bf16),
+            pltpu.VMEM((n_dp, block_rows), jnp.int32),
+            pltpu.VMEM((2, lead, block_rows, lanes), jnp.int32),
+            pltpu.VMEM((n_dp, lanes), jnp.float32),
+            pltpu.VMEM((n_dp - 1, n_dp, lanes), jnp.float32),
+            pltpu.VMEM((n_dp, chunk_rows, lanes), jnp.float32),
+            pltpu.VMEM((n_dp, lanes), jnp.float32),
+            pltpu.VMEM((n_expert - 1, n_dp, lanes), jnp.float32),
+            pltpu.VMEM((lead, block_rows, hidden), bf16),
+            pltpu.VMEM((lead - 1, block_rows, hidden), bf16),
+            pltpu.VMEM((block_rows, hidden), jnp.int16),
+            pltpu.VMEM((n_expert - 1, block_rows, hidden), jnp.int16),
+            dma((n_dp,)),
+            dma((chunks,)),
+            dma((chunks,)),
+            dma((lead - 1, chunks)),
+            dma((lead - 1, chunks)),
+            dma((n_expert - 1, chunks)),
+            dma((n_expert - 1, chunks)),
+            dma((n_dp - 1,)),
+            dma((n_dp - 1,)),
+            dma,
+            dma,
+            dma((n_expert - 1,)),
+            dma((n_expert - 1,)),
+        ],
+        compiler_params=pltpu.CompilerParams(collective_id=0, has_side_effects=True),
+    )(slot_expert, grads, offs)
+    return pl.pallas_call(
+        functools.partial(apply_kernel, n_dp),
+        out_shape=(
+            jax.ShapeDtypeStruct(master_weight.shape, jnp.float32),
+            jax.ShapeDtypeStruct(master_weight.shape, jnp.float32),
+            jax.ShapeDtypeStruct((1, 1), jnp.float32),
+        ),
+        in_specs=[vmem, vmem, vmem],
+        out_specs=(vmem, vmem, vmem),
+    )(totals, steps, master_weight)
+
+
 def solution(mesh):
+    n_dp = mesh.shape["dp"]
+    n_expert = mesh.shape["expert"]
+
+    def routed(expert_grads, round_offsets, slot_expert, master_weight):
+        slot_count, row_count, hidden = expert_grads.shape[1:]
+        block_rows = row_count // n_dp
+        fits = (
+            slot_count == 1
+            and n_expert > 1
+            and n_dp >= 4
+            and n_dp % 2 == 0
+            and block_rows == lanes
+            and hidden % lanes == 0
+        )
+        if fits:
+            return exchange_body(
+                n_dp, n_expert, expert_grads, round_offsets, slot_expert, master_weight
+            )
+        return body(expert_grads, round_offsets, slot_expert, master_weight)
+
     return jax.shard_map(
-        body,
+        routed,
         mesh=mesh,
         in_specs=(
             P("dp", "expert", None, None),

time: 171 us -> 41.3 us (0.24)
  waiting for transfers between devices: 107 us -> 0 us
  Pallas kernels: 0 us -> 40.4 us
  blocking collectives: 29.3 us -> 0 us
  between operations: 17.4 us -> 0.64 us
  other arithmetic: 13.5 us -> 0 us
  local copies, waits for them, and re-layouts: 3.84 us -> 0 us
    unnamed x3 -> x0, waiting for transfers between devices: 97.2 us -> none
    pallas_call x0 -> x2, Pallas kernels: none -> 40.4 us  [the longest x1 38.2 us: exchange_body(): pl.pallas_call(functools.partial(exchange_kernel, n_dp, n_expert), out_sh...]
    pmax x1 -> x0, blocking collectives: 23.2 us -> none  [body(): maxima = lax.pmax(block_peaks(local_grads, dp_count), 'dp')]
    all_gather x1 -> x0, waiting for transfers between devices: 9.31 us -> none  [body(): lax.all_gather(mean_slot, 'expert', axis=0, tiled=True)]
    unnamed x1 -> x0, blocking collectives: 6.11 us -> none
    convert_element_type x1 -> x0, other arithmetic: 4.18 us -> none  [quantize(): (floor_part + jnp.floor(scaled - floor_part + dither(element_code))).asty...]
    unnamed x13 -> x0, local copies, waits for them, and re-layouts: 3.18 us -> none
    sub x2 -> x0, other arithmetic: 3 us -> none  [the longest x1 2 us: body(): new_weight = master_weight - learn_rate * mean_grad]
  transfers between devices with their start and end apart: 2 -> 0, of which waited for: 2 -> 0; matrix products, arithmetic and copies ran while one was open for 3% -> 0% of each run, Pallas kernels for 0% -> 0%
where the time goes in v1:
time: 41.3 us; the launch traced here: 41.1 us
  Pallas kernels  40.4 us (98%)
  between operations  0.64 us (2%)
    pallas_call x1, Pallas kernels, exchange_body(): pl.pallas_call(functools.partial(exchange_kernel, n_dp, n_expert), out_sh...  38.2 us
    pallas_call x1, Pallas kernels, exchange_body(): pl.pallas_call(functools.partial(apply_kernel, n_dp), out_shape=(jax.Shap...  2.17 us

profile of v1, /device:TPU:0, one launch (start us, length us, event | category | flops | bytes accessed | tf_op | source)
XLA Modules:
  0.0 41.1 jit_solution(11434170421783925857)
XLA Ops:
  0.6 38.2 %shard_map.67 = (f32[128,896]{1,0:T(8,128)}, f32[8,128]{1,0:T(8,128)}) custom-call(s32[4]{0:T(128)} %slots_ref.1, bf16[4,2,128,896]{3,2,1,0:T(8,128)(2,1)} %bitcast.2, s32[8,128]{1,0:T(8,128)} %bitcast.3), custom_call_target="tpu_custom_call" | custom-call | tf_op jit(solution)/shard_map/pallas_call | solution.py:373
  38.9 2.2 %shard_map.68 = (f32[1,128,896]{2,1,0:T(8,128)}, f32[1,128,896]{2,1,0:T(8,128)}, f32[1,1]{1,0:T(1,128)}) custom-call(f32[128,896]{1,0:T(8,128)} %get-tuple-element.5.total_ref, f32[8,128]{1,0:T(8,128)} %get-tuple-element.6.step_ref, f32[1,128,896]{2,1,0:T(8,128)} %master_ref.1), custom_call_target="tpu_custom_call" | custom-call | tf_op jit(solution)/shard_map/pallas_call | solution.py:415

commit v2 on v1

--- a/solution.py
+++ b/solution.py
@@ -123,6 +123,12 @@
     z_in,
     x_out,
     x_in,
+    first_raw,
+    first_offs,
+    first_codes,
+    first_here,
+    first_out,
+    first_in,
     load_sem,
     y_send,
     y_recv,
@@ -136,10 +142,16 @@
     o_recv,
     s_send,
     s_recv,
+    f_send,
+    f_recv,
+    g_send,
+    g_recv,
+    p_send,
+    p_recv,
 ):
     lead = n_dp // 2
-    block_rows = own.shape[1]
-    hidden = own.shape[2]
+    block_rows = own.shape[2]
+    hidden = own.shape[3]
     tiles = hidden // lanes
     chunks = block_rows // chunk_rows
     me = lax.axis_index("dp")
@@ -162,7 +174,7 @@
 
     def load_copy(b):
         return pltpu.make_async_copy(
-            grads_ref.at[lax.div(b, 2), lax.rem(b, 2)], own.at[b], load_sem.at[b]
+            grads_ref.at[b // 2, b % 2], own.at[b // 2, b % 2], load_sem.at[b]
         )
 
     def remote(src, dst, send, recv, dp, expert):
@@ -175,15 +187,48 @@
             device_id_type=MESH,
         )
 
-    def y_copy(c):
-        return remote(
-            grads_ref.at[:, 1 - side, rows_of(c), :],
-            peer_raw.at[c],
-            y_send.at[c],
-            y_recv.at[c],
+    def y_copy(d, c):
+        return remote(
+            own.at[row_peer(d), 1 - side, rows_of(c), :],
+            peer_raw.at[c, d],
+            y_send.at[d, c],
+            y_recv.at[d, c],
             partner,
             mine,
         )
+
+    def first_copy(d):
+        return remote(
+            own.at[row_peer(d), :, rows_of(0), :],
+            first_raw.at[d - 1],
+            f_send.at[d - 1],
+            f_recv.at[d - 1],
+            row_peer(d) * 2 + side,
+            mine,
+        )
+
+    def first_offs_copy(d):
+        return remote(
+            offs_ref,
+            first_offs.at[d - 1],
+            g_send.at[d - 1],
+            g_recv.at[d - 1],
+            row_peer(d) * 2 + side,
+            mine,
+        )
+
+    p_copy = remote(first_out, first_in, p_send, p_recv, partner, mine)
+
+    remote_order = [lead // 2] + [d for d in range(1, lead) if d != lead // 2]
+
+    def y_issue(c):
+        for d in remote_order:
+            y_copy(d, c).start()
+        if c >= 3:
+            y_copy(0, c - 2).start()
+        if c == chunks - 1:
+            y_copy(0, c - 1).start()
+            y_copy(0, c).start()
 
     def z_copy(d, c):
         return remote(
@@ -231,7 +276,7 @@
         load_copy(b).wait()
 
         def peak_rows(i, peak):
-            return jnp.maximum(peak, jnp.abs(own[b, rows_of(i), :]))
+            return jnp.maximum(peak, jnp.abs(own[b // 2, b % 2, rows_of(i), :]))
 
         peak = lax.fori_loop(
             0, chunks, peak_rows, jnp.zeros((chunk_rows, hidden), own.dtype), unroll=True
@@ -244,8 +289,13 @@
     for d in range(1, n_dp):
         m_copy(d).start()
     o_copy.start()
-    for c in range(chunks):
-        y_copy(c).start()
+    for d in range(1, lead):
+        first_offs_copy(d).start()
+    for d in remote_order:
+        first_copy(d).start()
+    ahead = 4
+    for c in range(1, 1 + ahead):
+        y_issue(c)
 
     def spread(source, slot):
         lines = source[...]
@@ -257,6 +307,16 @@
     spread(offs_ref, 0)
     o_copy.wait_recv()
     spread(peer_offs, 1)
+
+    def first_spread(source, slot):
+        for at in range(2):
+            line = jnp.sum(
+                jnp.where(block_of_row == 2 * row + at, source, 0), axis=0, keepdims=True
+            )
+            column = jnp.transpose(jnp.broadcast_to(line, (lanes, block_rows)))[:chunk_rows]
+            first_codes[slot, at] = column * 747796405 + 1013904223
+
+    first_spread(offs_ref[...], 0)
 
     peak = my_max[...]
     for d in range(1, n_dp):
@@ -280,22 +340,50 @@
         wide = jnp.concatenate([code] * tiles, axis=1)
         return floor_part + jnp.floor((scaled - floor_part) + mixed_dither(wide + columns))
 
+    def round_piece(d, c):
+        y_copy(d, c).wait_recv()
+        k = row_peer(d)
+        inv_row = jnp.concatenate([inverse[2 * k + side]] * tiles, axis=1)
+        here = quantized(own[k, side, rows_of(c), :], inv_row, codes[0, k, rows_of(c), :])
+        there = quantized(peer_raw[c, d], inv_row, codes[1, k, rows_of(c), :])
+        stage[d, rows_of(c), :] = (here + there).astype(stage.dtype)
+
     def round_and_send(c):
-        y_copy(c).wait_recv()
-
-        def one(i, carry):
-            d = lax.rem(i + 1, lead)
-            k = row_peer(d)
-            b = 2 * k + side
-            inv_row = jnp.concatenate([inverse[b]] * tiles, axis=1)
-            here = quantized(own[b, rows_of(c), :], inv_row, codes[0, k, rows_of(c), :])
-            there = quantized(peer_raw[c, k], inv_row, codes[1, k, rows_of(c), :])
-            stage[d, rows_of(c), :] = (here + there).astype(stage.dtype)
-            return carry
-
-        lax.fori_loop(0, lead, one, 0)
+        last = None
+        for d in remote_order:
+            round_piece(d, c)
+            if last is not None:
+                z_copy(last, c).start()
+            last = d
+        if c >= 4:
+            round_piece(0, c - 3)
+        z_copy(last, c).start()
+
+    def first_round():
         for d in range(1, lead):
-            z_copy(d, c).start()
+            first_offs_copy(d).wait_recv()
+            first_spread(first_offs[d - 1], d)
+            first_copy(d).wait_recv()
+
+        def summed(at):
+            inv_row = jnp.concatenate([inverse[2 * row + at]] * tiles, axis=1)
+            total = quantized(own[row, at, rows_of(0), :], inv_row, first_codes[0, at])
+
+            def one(d, total):
+                return total + quantized(first_raw[d - 1, at], inv_row, first_codes[d, at])
+
+            return lax.fori_loop(1, lead, one, total)
+
+        first_out[...] = summed(1 - side).astype(first_out.dtype)
+        first_here[...] = summed(side)
+        p_copy.start()
+
+    def first_add():
+        p_copy.wait_recv()
+        total = first_here[...] + first_in[...].astype(jnp.float32)
+        x_out[rows_of(0), :] = total.astype(jnp.int32).astype(x_out.dtype)
+        for d in range(1, n_expert):
+            x_copy(d, 0).start()
 
     def add_and_send(c):
         total = stage[0, rows_of(c), :].astype(jnp.float32)
@@ -319,18 +407,26 @@
             chosen = chosen + part * weights[d]
         total_ref[rows_of(c), :] = chosen
 
-    lag_add = min(2, chunks)
-    lag_select = min(3, chunks)
-    for t in range(chunks + lag_select):
+    for t in range(1, chunks + 5):
         if t < chunks:
             round_and_send(t)
-        if t == 0:
+            if t + ahead < chunks:
+                y_issue(t + ahead)
+        elif t - 3 < chunks:
+            round_piece(0, t - 3)
+        if t == 1:
             for d in range(1, n_expert):
                 s_copy(d).start()
-        if 0 <= t - lag_add < chunks:
-            add_and_send(t - lag_add)
-        if 0 <= t - lag_select < chunks:
-            select(t - lag_select)
+        if t == 3:
+            first_round()
+        if 1 <= t - 3 < chunks:
+            add_and_send(t - 3)
+        if t == 6:
+            first_add()
+        if 1 <= t - 5 < chunks:
+            select(t - 5)
+        if t == 8:
+            select(0)
 
     chosen_step = my_step[...] * weights[0]
     for d in range(1, n_expert):
@@ -344,10 +440,16 @@
     o_copy.wait_send()
     for d in range(1, n_expert):
         s_copy(d).wait_send()
+    p_copy.wait_send()
+    for d in range(1, lead):
+        first_copy(d).wait_send()
+        first_offs_copy(d).wait_send()
     for c in range(chunks):
-        y_copy(c).wait_send()
-        for d in range(1, lead):
-            z_copy(d, c).wait_send()
+        for d in range(lead):
+            if c > 0:
+                y_copy(d, c).wait_send()
+            if c > 0 and d > 0:
+                z_copy(d, c).wait_send()
         for d in range(1, n_expert):
             x_copy(d, c).wait_send()
 
@@ -378,12 +480,12 @@
         ),
         in_specs=[
             pl.BlockSpec(memory_space=pltpu.SMEM),
-            pl.BlockSpec(memory_space=pl.ANY),
+            pl.BlockSpec(memory_space=pltpu.HBM),
             vmem,
         ],
         out_specs=(vmem, vmem),
         scratch_shapes=[
-            pltpu.VMEM((n_dp, block_rows, hidden), bf16),
+            pltpu.VMEM((lead, 2, block_rows, hidden), bf16),
             pltpu.VMEM((chunks, lead, chunk_rows, hidden), bf16),
             pltpu.VMEM((n_dp, block_rows), jnp.int32),
             pltpu.VMEM((2, lead, block_rows, lanes), jnp.int32),
@@ -396,9 +498,15 @@
             pltpu.VMEM((lead - 1, block_rows, hidden), bf16),
             pltpu.VMEM((block_rows, hidden), jnp.int16),
             pltpu.VMEM((n_expert - 1, block_rows, hidden), jnp.int16),
+            pltpu.VMEM((lead - 1, 2, chunk_rows, hidden), bf16),
+            pltpu.VMEM((lead - 1, n_dp, block_rows), jnp.int32),
+            pltpu.VMEM((lead, 2, chunk_rows, lanes), jnp.int32),
+            pltpu.VMEM((chunk_rows, hidden), jnp.float32),
+            pltpu.VMEM((chunk_rows, hidden), bf16),
+            pltpu.VMEM((chunk_rows, hidden), bf16),
             dma((n_dp,)),
-            dma((chunks,)),
-            dma((chunks,)),
+            dma((lead, chunks)),
+            dma((lead, chunks)),
             dma((lead - 1, chunks)),
             dma((lead - 1, chunks)),
             dma((n_expert - 1, chunks)),
@@ -409,8 +517,16 @@
             dma,
             dma((n_expert - 1,)),
             dma((n_expert - 1,)),
+            dma((lead - 1,)),
+            dma((lead - 1,)),
+            dma((lead - 1,)),
+            dma((lead - 1,)),
+            dma,
+            dma,
         ],
-        compiler_params=pltpu.CompilerParams(collective_id=0, has_side_effects=True),
+        compiler_params=pltpu.CompilerParams(
+            collective_id=0, has_side_effects=True
+        ),
     )(slot_expert, grads, offs)
     return pl.pallas_call(
         functools.partial(apply_kernel, n_dp),
@@ -436,6 +552,7 @@
             and n_expert > 1
             and n_dp >= 4
             and n_dp % 2 == 0
+            and n_dp <= 8
             and block_rows == lanes
             and hidden % lanes == 0
         )

time: 41.3 us -> 39.8 us (0.964)
  Pallas kernels: 40.4 us -> 38.9 us
    pallas_call x1, Pallas kernels: 38.2 us -> 36.7 us  [exchange_body(): pl.pallas_call(functools.partial(exchange_kernel, n_dp, n_expert), out_sh...]
where the time goes in v2:
time: 39.8 us; the launch traced here: 39.6 us
  Pallas kernels  38.9 us (98%)
  between operations  0.64 us (2%)
    pallas_call x1, Pallas kernels, exchange_body(): pl.pallas_call(functools.partial(exchange_kernel, n_dp, n_expert), out_sh...  36.7 us
    pallas_call x1, Pallas kernels, exchange_body(): pl.pallas_call(functools.partial(apply_kernel, n_dp), out_shape=(jax.Shap...  2.17 us

profile of v2, /device:TPU:0, one launch (start us, length us, event | category | flops | bytes accessed | tf_op | source)
XLA Modules:
  0.0 39.6 jit_solution(4895358774944164790)
XLA Ops:
  0.6 36.7 %shard_map.67 = (f32[128,896]{1,0:T(8,128)}, f32[8,128]{1,0:T(8,128)}) custom-call(s32[4]{0:T(128)} %slots_ref.1, bf16[4,2,128,896]{3,2,1,0:T(8,128)(2,1)} %bitcast.2, s32[8,128]{1,0:T(8,128)} %bitcast.3), custom_call_target="tpu_custom_call" | custom-call | tf_op jit(solution)/shard_map/pallas_call | solution.py:475
  37.4 2.2 %shard_map.68 = (f32[1,128,896]{2,1,0:T(8,128)}, f32[1,128,896]{2,1,0:T(8,128)}, f32[1,1]{1,0:T(1,128)}) custom-call(f32[128,896]{1,0:T(8,128)} %get-tuple-element.5.total_ref, f32[8,128]{1,0:T(8,128)} %get-tuple-element.6.step_ref, f32[1,128,896]{2,1,0:T(8,128)} %master_ref.1), custom_call_target="tpu_custom_call" | custom-call | tf_op jit(solution)/shard_map/pallas_call | solution.py:531
